TPU v7x, 32 devices: a whole 2x2x4 slice. The times are simulated.
32 devices in a mesh: dp: 2 (over y), row: 4 (over x, core), col: 4 (over z).
Axes of the slice: x: 2, y: 2, z: 4, core: 2. Of those that a mesh axis runs over, the one named last changes fastest.
Arguments:
- tokens: bfloat16 [2048, 8192], P(('dp', 'col'), 'row'), may hold values from -6 to 6
- frozen_weight: bfloat16 [8192, 8192], P('row', 'col'), may hold values from -0.0625 to 0.0625
- input_adapter_factor: bfloat16 [16, 8192], P(None, 'row'), may hold values from -0.0625 to 0.0625
- output_adapter_factor: bfloat16 [16, 8192], P(None, 'col'), may hold values from -1.5 to 1.5
- magnitude: float32 [8192], P('col'), may hold values from 0.5 to 2
- cotangent: bfloat16 [2048, 8192], P(('dp', 'row'), 'col'), may hold values from -6 to 6
- sequence_lengths: int32 [2, 8], P('dp'), may hold values from 1 to 512, 1024 in all within a row
Outputs:
- projected: bfloat16 [2048, 8192], P(('dp', 'row'), 'col')
- grad_mag: float32 [8192], P('col')
- input_factor_gradient: float32 [16, 8192], P(None, 'row')
- grad_b: float32 [16, 8192], P(None, 'col')
Inputs may be any that keep to these rules, and one draw needn't show every extreme that they name: `sequence_lengths`: each group's 8 lengths sum to 1024, and one of them is exactly 512.
All inputs are finite; a program needn't handle non-finite values.
Results may differ from a plain program's by a relative error of at most 0.0052.
Values may be sent and summed in bfloat16 or wider, within the bound.
No kernel may reach another device: no remote copies, remote signals or barrier semaphores. Data moves between devices by JAX's collectives and lax.ppermute only.
A program may use at most 64 MiB of HBM per device.

v0:
```python
import jax
import jax.numpy as jnp
from jax import lax
from jax.sharding import PartitionSpec as P

norm_eps = 1e-06
highest_precision = lax.Precision.HIGHEST


def contract_product(left, right, left_dim, right_dim):
    return lax.dot_general(
        left, right, (((left_dim,), (right_dim,)), ((), ())), preferred_element_type=jnp.float32
    )


def per_device(
    tokens,
    frozen_weight,
    input_adapter_factor,
    output_adapter_factor,
    magnitude,
    cotangent,
    sequence_lengths,
):
    row_count = lax.axis_size("row")
    col_count = lax.axis_size("col")
    row_index = lax.axis_index("row")
    col_index = lax.axis_index("col")
    group_index = lax.axis_index("dp")
    local_rows = tokens.shape[0]
    group_rows = local_rows * col_count
    block_rows = group_rows // row_count
    adapter_rank_size = input_adapter_factor.shape[0]
    low_rank_update = contract_product(input_adapter_factor, output_adapter_factor, 0, 0)
    merged = frozen_weight.astype(jnp.float32) + low_rank_update
    norm_terms = jnp.sum(merged * merged, axis=0)
    gram_partial_terms = contract_product(input_adapter_factor, input_adapter_factor, 1, 1)
    merged_factor_terms = jnp.dot(
        input_adapter_factor, frozen_weight, preferred_element_type=jnp.float32
    ) + jnp.dot(
        gram_partial_terms, output_adapter_factor.astype(jnp.float32), precision=highest_precision
    )
    portion = lax.all_gather(tokens, "col", axis=0, tiled=True)
    base_piece = jnp.dot(portion, frozen_weight, preferred_element_type=jnp.float32)
    down_portion = contract_product(portion, input_adapter_factor, 1, 1)
    frozen_rows, down_rows = (
        lax.psum_scatter(base_piece, "row", scatter_dimension=0, tiled=True),
        lax.psum_scatter(down_portion, "row", scatter_dimension=0, tiled=True),
    )
    norm_sq, merged_input_factor = lax.psum((norm_terms, merged_factor_terms), "row")
    down_activations = down_rows.astype(jnp.bfloat16)
    col_norm = jnp.sqrt(norm_sq + norm_eps)
    col_scale = magnitude / col_norm
    query_projection = frozen_rows + jnp.dot(
        down_activations, output_adapter_factor, preferred_element_type=jnp.float32
    )
    projected = (query_projection * col_scale[None, :]).astype(jnp.bfloat16)
    lengths = sequence_lengths[0]
    ends = jnp.cumsum(lengths, dtype=jnp.int32)
    starts = ends - lengths
    positions = row_index * block_rows + jnp.arange(block_rows, dtype=jnp.int32)
    inside = (positions[:, None] >= starts[None, :]) & (positions[:, None] < ends[None, :])
    inverse = 1.0 / lengths.astype(jnp.float32)
    weights = jnp.sum(jnp.where(inside, inverse[None, :], jnp.float32(0.0)), axis=1)
    grad_out = cotangent.astype(jnp.float32) * weights[:, None]
    scale_terms = jnp.sum(grad_out * query_projection, axis=0)
    projection_gradient = (grad_out * col_scale[None, :]).astype(jnp.bfloat16)
    bgrad_terms = contract_product(down_activations, projection_gradient, 0, 0)
    scale_grad, bgrad_data = lax.psum((scale_terms, bgrad_terms), ("dp", "row"))
    grad_mag = scale_grad / col_norm
    norm_coefficient = -scale_grad * magnitude / (col_norm * col_norm * col_norm)
    grad_b = bgrad_data + merged_input_factor * norm_coefficient[None, :]
    backward_terms = contract_product(projection_gradient, output_adapter_factor, 1, 1)
    padded = lax.dynamic_update_slice_in_dim(
        jnp.zeros((group_rows, adapter_rank_size), jnp.float32),
        backward_terms,
        row_index * block_rows,
        0,
    )
    backward_rows = lax.psum(padded, ("row", "col")).astype(jnp.bfloat16)
    back_mine = lax.dynamic_slice_in_dim(backward_rows, col_index * local_rows, local_rows, 0)
    row_term = contract_product(back_mine, tokens, 0, 0)
    scaled_output_factor = (
        output_adapter_factor.astype(jnp.float32) * norm_coefficient[None, :]
    ).astype(jnp.bfloat16)
    norm_term = contract_product(scaled_output_factor, frozen_weight, 1, 1) + jnp.dot(
        contract_product(scaled_output_factor, output_adapter_factor, 1, 1),
        input_adapter_factor.astype(jnp.float32),
        precision=highest_precision,
    )
    first_group = (group_index == 0).astype(jnp.float32)
    input_factor_gradient = lax.psum(row_term + first_group * norm_term, ("dp", "col"))
    return (projected, grad_mag, input_factor_gradient, grad_b)


def solution(mesh):
    in_specs = (
        P(("dp", "col"), "row"),
        P("row", "col"),
        P(None, "row"),
        P(None, "col"),
        P("col"),
        P(("dp", "row"), "col"),
        P("dp", None),
    )
    out_specs = (P(("dp", "row"), "col"), P("col"), P(None, "row"), P(None, "col"))
    return jax.shard_map(
        per_device, mesh=mesh, in_specs=in_specs, out_specs=out_specs, check_vma=False
    )
```

profile of v0, /device:TPU:0, one launch (start us, length us, event | category | flops | bytes accessed | tf_op | source)
XLA Modules:
  0.0 366.2 jit_solution(13270679273868545477)
XLA Ops:
  7.2 0.0 copy-start
  7.2 0.0 all-gather.2.cloned.1.call-start
  7.2 0.7 all-gather.2.cloned.1.call-update
  7.9 0.0 reduce-scatter.5.cloned.1.call-start
  8.0 85.1 %all-gather.2.cloned.1.call-done = bf16[1024,2048]{1,0:T(8,128)(2,1)} async-done(((bf16[256,2048]{1,0:T(8,128)(2,1)}), bf16[1024,2048]{1,0:T(8,128)(2,1)}) %all-gather.2.cloned.1.call-update) | async-done | bytes 4194320 | tf_op jit(solution)/shard_map/all_gather | solution.py:43
  93.1 0.0 copy-done
  93.1 4.0 %fusion.14 = f32[1024,16]{0,1:T(8,128)} fusion(bf16[1024,2048]{1,0:T(8,128)(2,1)} %all-gather.2.cloned.1.call-done, bf16[16,2048]{1,0:T(8,128)(2,1)S(1)} %copy-done), kind=kOutput, calls=%fused_computation.33 | convolution fusion | flops 67108864 | bytes 4325376 | tf_op jit(solution)/shard_map/dot_general | solution.py:11
  97.1 0.0 reduce-scatter.5.cloned.1.call-update
  97.1 0.0 reduce-scatter.3.cloned.1.call-start
  97.1 14.4 %fusion.13 = f32[1024,2048]{1,0:T(8,128)} fusion(bf16[1024,2048]{1,0:T(8,128)(2,1)} %all-gather.2.cloned.1.call-done, bf16[2048,2048]{1,0:T(8,128)(2,1)} %param.8), kind=kOutput, calls=%fused_computation.32 | convolution fusion | flops 8589934592 | bytes 20971520 | tf_op jit(solution)/shard_map/dot_general | solution.py:44
  111.6 0.0 reduce-scatter.3.cloned.1.call-update
  111.6 0.0 all-reduce.8.cloned.1.call-start
  111.6 0.1 fusion.16
  111.8 0.0 copy-start.2
  111.8 4.6 %fusion.15 = f32[16,2048]{1,0:T(8,128)S(1)} fusion(bf16[16,2048]{1,0:T(8,128)(2,1)S(1)} %copy-done, bf16[2048,2048]{1,0:T(8,128)(2,1)} %param.8), kind=kOutput, calls=%fused_computation.34 | convolution fusion | flops 134217728 | bytes 8585216 | tf_op jit(solution)/shard_map/dot_general | solution.py:38
  116.4 0.0 copy-done.2
  116.4 0.9 convolution_add_fusion.1
  117.3 0.0 all-reduce.8.cloned.1.call-update
  117.3 0.0 all-reduce.6.cloned.1.call-start
  117.3 0.0 copy-start.5
  117.4 0.0 copy-start.4
  117.4 0.0 copy-start.3
  117.4 5.9 %multiply_reduce_fusion = f32[2048]{0:T(1024)S(1)} fusion(bf16[2048,2048]{1,0:T(8,128)(2,1)} %param.8, bf16[16,2048]{1,0:T(8,128)(2,1)S(1)} %copy-done, bf16[16,2048]{1,0:T(8,128)(2,1)S(1)} %copy-done.2), kind=kOutput, calls=%fused_computation | convolution fusion | flops 150992896 | bytes 8527872 | tf_op jit(solution)/shard_map/dot_general | solution.py:11
  123.3 0.0 copy-done.5
  123.3 0.2 reduce-window.4
  123.5 6.5 %psum.42 = f32[2048]{0:T(1024)S(1)} all-reduce(f32[2048]{0:T(1024)S(1)} %multiply_reduce_fusion), channel_id=1, replica_groups=mesh['dp'=2,'row'=4,'col'=4] {'row'}, use_global_device_ids=true, to_apply=%region_3.0 | all-reduce | flops 2048 | bytes 16384 | tf_op jit(solution)/shard_map/psum | solution.py:50
  130.0 0.0 copy-done.4
  130.1 0.1 select_reduce_fusion
  130.2 0.0 copy-done.3
  130.2 0.5 convolution_dynamic-update-slice_fusion
  130.7 69.2 %psum.44 = bf16[1024,16]{1,0:T(8,128)(2,1)S(1)} all-reduce(f32[1024,16]{1,0:T(8,128)S(1)} %convolution_dynamic-update-slice_fusion), channel_id=1, replica_groups=mesh['dp'=2,'row'=4,'col'=4] {'row','col'}, use_global_device_ids=true, to_apply=%region_8.9 | all-reduce | flops 16384 | bytes 98304 | tf_op jit(solution)/shard_map/psum | solution.py:80
  199.9 0.0 reduce-scatter.5.cloned.1.call-done
  200.0 1.8 fusion.1
  201.8 0.0 all-reduce.6.cloned.1.call-update
  201.8 0.0 all-reduce.4.cloned.1.call-start
  201.8 0.0 reduce-scatter.3.cloned.1.call-done
  201.9 3.2 multiply_reduce_fusion.1
  205.1 12.1 %psum.43 = f32[2048]{0:T(1024)S(1)} all-reduce(f32[2048]{0:T(1024)S(1)} %get-tuple-element.4), channel_id=1, replica_groups=mesh['dp'=2,'row'=4,'col'=4] {'dp','row'}, use_global_device_ids=true, to_apply=%region_7.8 | all-reduce | flops 2048 | bytes 16384 | tf_op jit(solution)/shard_map/psum | solution.py:69
  217.1 0.6 fusion.6
  217.8 0.0 copy-start.1
  217.8 5.7 %fusion.3 = f32[16,2048]{1,0:T(8,128)S(1)} fusion(bf16[2048,2048]{1,0:T(8,128)(2,1)} %param.8, bf16[16,2048]{1,0:T(8,128)(2,1)S(1)} %copy-done.2, f32[2048]{0:T(1024)S(1)} %get-tuple-element.6), kind=kOutput, calls=%fused_computation.16 | convolution fusion | flops 134316032 | bytes 8593408 | tf_op jit(solution)/shard_map/dot_general | solution.py:11
  223.5 0.1 fusion.2
  223.6 0.2 fusion
  223.9 0.0 copy-done.1
  223.9 0.9 convolution_add_fusion.3
  224.8 0.0 all-reduce.4.cloned.1.call-update
  224.8 2.4 all-reduce.8.cloned.1.call-done
  227.2 57.0 %all-reduce.6.cloned.1.call-done = f32[16,2048]{1,0:T(8,128)} async-done(((f32[16,2048]{1,0:T(8,128)}), f32[16,2048]{1,0:T(8,128)}) %all-reduce.6.cloned.1.call-update) | async-done | bytes 131088 | tf_op jit(solution)/shard_map/psum | solution.py:69
  284.2 1.6 multiply_add_fusion
  285.9 71.9 %all-reduce.4.cloned.1.call-done = f32[16,2048]{1,0:T(8,128)} async-done(((f32[16,2048]{1,0:T(8,128)}), f32[16,2048]{1,0:T(8,128)}) %all-reduce.4.cloned.1.call-update) | async-done | bytes 131088 | tf_op jit(solution)/shard_map/psum | solution.py:92
  357.8 1.6 copy.15
  (5 shorter events, 0.1 us)
Async XLA Ops:
  7.2 85.9 %copy-start = (bf16[16,2048]{1,0:T(8,128)(2,1)S(1)}, bf16[16,2048]{1,0:T(8,128)(2,1)}, u32[]{:S(2)}) copy-start(bf16[16,2048]{1,0:T(8,128)(2,1)} %param.9) | copy-start | bytes 196612
  7.2 85.9 %all-gather.2.cloned.1.call-start = ((), (), s32[]{:S(2)}) async-start(), calls=%async_computation.2 | async-start | bytes 5242880 | tf_op jit(solution)/shard_map/all_gather | solution.py:43
  7.9 192.0 %reduce-scatter.5.cloned.1.call-start = ((), (), s32[]{:S(2)}) async-start(), calls=%async_computation.4 | async-start | bytes 81920 | tf_op jit(solution)/shard_map/reduce_scatter | solution.py:48
  97.1 104.8 %reduce-scatter.3.cloned.1.call-start = ((), (), s32[]{:S(2)}) async-start(), calls=%async_computation.3 | async-start | bytes 10485760 | tf_op jit(solution)/shard_map/reduce_scatter | solution.py:47
  111.6 115.7 %all-reduce.8.cloned.1.call-start = ((), (), s32[]{:S(2)}) async-start(), calls=%async_computation.7 | async-start | bytes 262144 | tf_op jit(solution)/shard_map/psum | solution.py:50
  111.8 4.6 %copy-start.2 = (bf16[16,2048]{1,0:T(8,128)(2,1)S(1)}, bf16[16,2048]{1,0:T(8,128)(2,1)}, u32[]{:S(2)}) copy-start(bf16[16,2048]{1,0:T(8,128)(2,1)} %param.10) | copy-start | bytes 196612
  117.3 166.9 %all-reduce.6.cloned.1.call-start = ((), (), s32[]{:S(2)}) async-start(), calls=%async_computation.6 | async-start | bytes 262144 | tf_op jit(solution)/shard_map/psum | solution.py:69
  117.3 5.9 %copy-start.5 = (s32[1,8]{1,0:T(1,128)S(1)}, s32[1,8]{1,0:T(1,128)}, u32[]{:S(2)}) copy-start(s32[1,8]{1,0:T(1,128)} %param.13) | copy-start | bytes 100
  117.4 12.7 %copy-start.4 = (f32[2048]{0:T(1024)S(1)}, f32[2048]{0:T(1024)}, u32[]{:S(2)}) copy-start(f32[2048]{0:T(1024)} %param.11) | copy-start | bytes 24580
  117.4 12.8 %copy-start.3 = (bf16[256,2048]{1,0:T(8,128)(2,1)S(1)}, bf16[256,2048]{1,0:T(8,128)(2,1)}, u32[]{:S(2)}) copy-start(bf16[256,2048]{1,0:T(8,128)(2,1)} %param.12) | copy-start | bytes 3145732
  201.8 156.0 %all-reduce.4.cloned.1.call-start = ((), (), s32[]{:S(2)}) async-start(), calls=%async_computation.5 | async-start | bytes 262144 | tf_op jit(solution)/shard_map/psum | solution.py:92
  217.8 6.1 %copy-start.1 = (bf16[256,2048]{1,0:T(8,128)(2,1)S(1)}, bf16[256,2048]{1,0:T(8,128)(2,1)}, u32[]{:S(2)}) copy-start(bf16[256,2048]{1,0:T(8,128)(2,1)} %param.7) | copy-start | bytes 3145732
Sparse Core Ops, SparseCore 0:
  9.6 83.4 all-gather.1
  97.2 18.0 reduce-scatter.4
  117.9 75.6 reduce-scatter.2
  195.8 31.4 all-reduce.7
  230.7 53.4 all-reduce.5
  288.0 69.7 all-reduce.3
where the time goes:
time: 367 us; the launch traced here: 366 us
  waiting for transfers between devices  217 us (59%)
  blocking collectives  87.8 us (24%)
  matrix products  42.5 us (12%)
  between operations  14.3 us (4%)
    all_gather x1, waiting for transfers between devices, per_device(): portion = lax.all_gather(tokens, 'col', axis=0, tiled=True)  85.1 us
    psum x1, waiting for transfers between devices, per_device(): lax.psum(row_term + first_group * norm_term, ('dp', 'col'))  71.9 us
    psum x1, blocking collectives, per_device(): backward_rows = lax.psum(padded, ('row', 'col')).astype(jnp.bfloat16)  69.2 us
    psum x1, waiting for transfers between devices, per_device(): scale_grad, bgrad_data = lax.psum((scale_terms, bgrad_terms), ('dp', 'row'))  57 us
    dot_general x8, matrix products, contract_product(): lax.dot_general(left, right, (((left_dim,), (right_dim,)), ((), ())), pre...  19.1 us
    dot_general x1, matrix products, per_device(): jnp.dot(portion, frozen_weight, preferred_element_type=jnp.float32)  14.4 us
    psum x1, blocking collectives, per_device(): scale_grad, bgrad_data = lax.psum((scale_terms, bgrad_terms), ('dp', 'row'))  12.1 us
  transfers between devices with their start and end apart: 6, of which 4 were waited for; matrix products, arithmetic and copies ran while one was open for 11% of the time, Pallas kernels for 0%

commit v1 on v0

--- a/solution.py
+++ b/solution.py
@@ -77,7 +77,7 @@
         row_index * block_rows,
         0,
     )
-    backward_rows = lax.psum(padded, ("row", "col")).astype(jnp.bfloat16)
+    backward_rows = jnp.sum(lax.all_gather(padded, ("row", "col")), axis=0).astype(jnp.bfloat16)
     back_mine = lax.dynamic_slice_in_dim(backward_rows, col_index * local_rows, local_rows, 0)
     row_term = contract_product(back_mine, tokens, 0, 0)
     scaled_output_factor = (

time: 367 us -> 401 us (1.093)
  waiting for transfers between devices: 217 us -> 316 us
  blocking collectives: 87.8 us -> 21.3 us
    reduce_scatter x1, waiting for transfers between devices: 0.02 us -> 72 us  [per_device(): lax.psum_scatter(base_piece, 'row', scatter_dimension=0, tiled=True)]
    psum x1 -> x0, blocking collectives: 69.2 us -> none  [per_device(): backward_rows = lax.psum(padded, ('row', 'col')).astype(jnp.bfloat16)]
    reduce_scatter x1, waiting for transfers between devices: 0.02 us -> 20.3 us  [per_device(): lax.psum_scatter(down_portion, 'row', scatter_dimension=0, tiled=True)]
    all_gather x1, waiting for transfers between devices: 85.1 us -> 68.4 us  [per_device(): portion = lax.all_gather(tokens, 'col', axis=0, tiled=True)]
    all_gather x0 -> x1, waiting for transfers between devices: none -> 14.9 us  [per_device(): lax.all_gather(padded, ('row', 'col'))]
    psum x1, waiting for transfers between devices: 2.4 us -> 10.3 us  [per_device(): lax.psum((norm_terms, merged_factor_terms), 'row')]
  transfers between devices with their start and end apart: 6 -> 7, of which waited for: 4 -> 7; matrix products, arithmetic and copies ran while one was open for 11% -> 12% of each run, Pallas kernels for 0% -> 0%
where the time goes in v1:
time: 401 us
  waiting for transfers between devices  316 us (79%)
  matrix products  42.4 us (11%)
  blocking collectives  21.3 us (5%)
  between operations  14.3 us (4%)
  other arithmetic  4.48 us (1%)
    psum x1, waiting for transfers between devices, per_device(): lax.psum(row_term + first_group * norm_term, ('dp', 'col'))  72.1 us
    reduce_scatter x1, waiting for transfers between devices, per_device(): lax.psum_scatter(base_piece, 'row', scatter_dimension=0, tiled=True)  72 us
    all_gather x1, waiting for transfers between devices, per_device(): portion = lax.all_gather(tokens, 'col', axis=0, tiled=True)  68.4 us
    psum x1, waiting for transfers between devices, per_device(): scale_grad, bgrad_data = lax.psum((scale_terms, bgrad_terms), ('dp', 'row'))  57 us
    reduce_scatter x1, waiting for transfers between devices, per_device(): lax.psum_scatter(down_portion, 'row', scatter_dimension=0, tiled=True)  20.3 us
    dot_general x8, matrix products, contract_product(): lax.dot_general(left, right, (((left_dim,), (right_dim,)), ((), ())), pre...  19.1 us
    all_gather x1, waiting for transfers between devices, per_device(): lax.all_gather(padded, ('row', 'col'))  14.9 us
    dot_general x1, matrix products, per_device(): jnp.dot(portion, frozen_weight, preferred_element_type=jnp.float32)  14.4 us
  transfers between devices with their start and end apart: 7, of which 7 were waited for; matrix products, arithmetic and copies ran while one was open for 12% of the time, Pallas kernels for 0%

profile of v1, /device:TPU:0, one launch (start us, length us, event | category | flops | bytes accessed | tf_op | source)
XLA Modules:
  0.0 400.8 jit_solution(7943701640903856582)
XLA Ops:
  7.2 0.0 copy-start
  7.2 0.0 all-gather.3.cloned.1.call-start
  7.2 0.7 all-gather.3.cloned.1.call-update
  7.9 0.0 all-gather.5.cloned.1.call-start
  8.0 0.8 reduce-window.4
  8.8 0.0 copy-done
  8.8 0.0 copy-start.6
  8.8 0.0 copy-start.5
  8.8 0.0 copy-start.2
  8.8 0.0 copy-start.3
  8.8 5.9 %multiply_reduce_fusion = f32[2048]{0:T(1024)S(1)} fusion(bf16[2048,2048]{1,0:T(8,128)(2,1)} %param.8, bf16[16,2048]{1,0:T(8,128)(2,1)S(1)} %copy-done, bf16[16,2048]{1,0:T(8,128)(2,1)} %param.10), kind=kOutput, calls=%fused_computation | convolution fusion | flops 150992896 | bytes 8527872 | tf_op jit(solution)/shard_map/dot_general | solution.py:11
  14.7 8.5 %psum.35 = f32[2048]{0:T(1024)S(1)} all-reduce(f32[2048]{0:T(1024)S(1)} %multiply_reduce_fusion), channel_id=1, replica_groups=mesh['dp'=2,'row'=4,'col'=4] {'row'}, use_global_device_ids=true, to_apply=%region_3.0 | all-reduce | flops 2048 | bytes 16384 | tf_op jit(solution)/shard_map/psum | solution.py:50
  23.3 0.0 copy-done.6
  23.3 0.1 select_reduce_fusion
  23.4 0.0 copy-done.5
  23.4 0.0 copy-done.2
  23.5 0.0 copy-done.3
  23.5 0.5 fusion.1
  23.9 0.0 copy-start.4
  23.9 0.6 copy-done.4
  24.6 0.0 all-gather.5.cloned.1.call-update
  24.6 0.0 reduce-scatter.5.cloned.1.call-start
  24.6 68.4 %all-gather.3.cloned.1.call-done = bf16[1024,2048]{1,0:T(8,128)(2,1)} async-done(((bf16[256,2048]{1,0:T(8,128)(2,1)}), bf16[1024,2048]{1,0:T(8,128)(2,1)}) %all-gather.3.cloned.1.call-update) | async-done | bytes 4194320 | tf_op jit(solution)/shard_map/all_gather | solution.py:43
  93.1 4.0 %fusion.15 = f32[1024,16]{0,1:T(8,128)} fusion(bf16[1024,2048]{1,0:T(8,128)(2,1)} %all-gather.3.cloned.1.call-done, bf16[16,2048]{1,0:T(8,128)(2,1)S(1)} %copy-done), kind=kOutput, calls=%fused_computation.34 | convolution fusion | flops 67108864 | bytes 4325376 | tf_op jit(solution)/shard_map/dot_general | solution.py:11
  97.1 0.0 reduce-scatter.5.cloned.1.call-update
  97.1 0.0 reduce-scatter.3.cloned.1.call-start
  97.1 14.4 %fusion.14 = f32[1024,2048]{1,0:T(8,128)} fusion(bf16[1024,2048]{1,0:T(8,128)(2,1)} %all-gather.3.cloned.1.call-done, bf16[2048,2048]{1,0:T(8,128)(2,1)} %param.8), kind=kOutput, calls=%fused_computation.33 | convolution fusion | flops 8589934592 | bytes 20971520 | tf_op jit(solution)/shard_map/dot_general | solution.py:44
  111.6 0.0 reduce-scatter.3.cloned.1.call-update
  111.6 0.0 all-reduce.8.cloned.1.call-start
  111.6 0.1 fusion.17
  111.8 4.6 %fusion.16 = f32[16,2048]{1,0:T(8,128)S(1)} fusion(bf16[16,2048]{1,0:T(8,128)(2,1)S(1)} %copy-done, bf16[2048,2048]{1,0:T(8,128)(2,1)} %param.8), kind=kOutput, calls=%fused_computation.35 | convolution fusion | flops 134217728 | bytes 8585216 | tf_op jit(solution)/shard_map/dot_general | solution.py:38
  116.4 0.8 convolution_add_fusion.1
  117.2 0.0 all-reduce.8.cloned.1.call-update
  117.2 0.0 all-reduce.6.cloned.1.call-start
  117.3 14.9 %all-gather.5.cloned.1.call-done = f32[16,1024,16]{1,2,0:T(8,128)} async-done(((f32[1,1024,16]{1,2,0:T(8,128)}), f32[16,1024,16]{1,2,0:T(8,128)}) %all-gather.5.cloned.1.call-update) | async-done | bytes 1048592 | tf_op jit(solution)/shard_map/all_gather | solution.py:80
  132.3 1.3 reduce_sum.39
  133.5 20.3 %reduce-scatter.5.cloned.1.call-done = f32[256,16]{0,1:T(8,128)} async-done(((f32[1024,16]{0,1:T(8,128)}), f32[256,16]{0,1:T(8,128)}) %reduce-scatter.5.cloned.1.call-update) | async-done | bytes 16400 | tf_op jit(solution)/shard_map/reduce_scatter | solution.py:48
  153.8 1.8 fusion.2
  155.6 0.0 all-reduce.6.cloned.1.call-update
  155.6 0.0 all-reduce.4.cloned.1.call-start
  155.7 72.0 %reduce-scatter.3.cloned.1.call-done = f32[256,2048]{1,0:T(8,128)} async-done(((f32[1024,2048]{1,0:T(8,128)}), f32[256,2048]{1,0:T(8,128)}) %reduce-scatter.3.cloned.1.call-update) | async-done | bytes 2097168 | tf_op jit(solution)/shard_map/reduce_scatter | solution.py:47
  227.7 3.2 multiply_reduce_fusion.1
  230.9 12.8 %psum.36 = f32[2048]{0:T(1024)S(1)} all-reduce(f32[2048]{0:T(1024)S(1)} %get-tuple-element.4), channel_id=1, replica_groups=mesh['dp'=2,'row'=4,'col'=4] {'dp','row'}, use_global_device_ids=true, to_apply=%region_7.8 | all-reduce | flops 2048 | bytes 16384 | tf_op jit(solution)/shard_map/psum | solution.py:69
  243.7 0.6 fusion.7
  244.3 0.0 copy-start.1
  244.3 5.7 %fusion.4 = f32[16,2048]{1,0:T(8,128)S(1)} fusion(bf16[2048,2048]{1,0:T(8,128)(2,1)} %param.8, bf16[16,2048]{1,0:T(8,128)(2,1)S(1)} %copy-done.2, f32[2048]{0:T(1024)S(1)} %get-tuple-element.6), kind=kOutput, calls=%fused_computation.16 | convolution fusion | flops 134316032 | bytes 8593408 | tf_op jit(solution)/shard_map/dot_general | solution.py:11
  250.1 0.1 fusion.3
  250.2 0.2 fusion
  250.4 0.0 copy-done.1
  250.5 0.9 convolution_add_fusion.3
  251.4 0.0 all-reduce.4.cloned.1.call-update
  251.4 10.3 %all-reduce.8.cloned.1.call-done = f32[16,2048]{1,0:T(8,128)} async-done(((f32[16,2048]{1,0:T(8,128)}), f32[16,2048]{1,0:T(8,128)}) %all-reduce.8.cloned.1.call-update) | async-done | bytes 131088 | tf_op jit(solution)/shard_map/psum | solution.py:50
  261.7 57.0 %all-reduce.6.cloned.1.call-done = f32[16,2048]{1,0:T(8,128)} async-done(((f32[16,2048]{1,0:T(8,128)}), f32[16,2048]{1,0:T(8,128)}) %all-reduce.6.cloned.1.call-update) | async-done | bytes 131088 | tf_op jit(solution)/shard_map/psum | solution.py:69
  318.7 1.6 multiply_add_fusion
  320.3 72.1 %all-reduce.4.cloned.1.call-done = f32[16,2048]{1,0:T(8,128)} async-done(((f32[16,2048]{1,0:T(8,128)}), f32[16,2048]{1,0:T(8,128)}) %all-reduce.4.cloned.1.call-update) | async-done | bytes 131088 | tf_op jit(solution)/shard_map/psum | solution.py:92
  392.4 1.6 copy.15
  (5 shorter events, 0.0 us)
Async XLA Ops:
  7.2 1.6 copy-start
  7.2 85.9 %all-gather.3.cloned.1.call-start = ((), (), s32[]{:S(2)}) async-start(), calls=%async_computation.2 | async-start | bytes 5242880 | tf_op jit(solution)/shard_map/all_gather | solution.py:43
  7.9 124.3 %all-gather.5.cloned.1.call-start = ((), (), s32[]{:S(2)}) async-start(), calls=%async_computation.5 | async-start | bytes 1114112 | tf_op jit(solution)/shard_map/all_gather | solution.py:80
  8.8 14.5 %copy-start.6 = (s32[1,8]{1,0:T(1,128)S(1)}, s32[1,8]{1,0:T(1,128)}, u32[]{:S(2)}) copy-start(s32[1,8]{1,0:T(1,128)} %param.13) | copy-start | bytes 100
  8.8 14.6 %copy-start.5 = (f32[2048]{0:T(1024)S(1)}, f32[2048]{0:T(1024)}, u32[]{:S(2)}) copy-start(f32[2048]{0:T(1024)} %param.11) | copy-start | bytes 24580
  8.8 14.6 %copy-start.2 = (bf16[16,2048]{1,0:T(8,128)(2,1)S(1)}, bf16[16,2048]{1,0:T(8,128)(2,1)}, u32[]{:S(2)}) copy-start(bf16[16,2048]{1,0:T(8,128)(2,1)} %param.10) | copy-start | bytes 196612
  8.8 14.6 %copy-start.3 = (bf16[256,2048]{1,0:T(8,128)(2,1)S(1)}, bf16[256,2048]{1,0:T(8,128)(2,1)}, u32[]{:S(2)}) copy-start(bf16[256,2048]{1,0:T(8,128)(2,1)} %param.12) | copy-start | bytes 3145732
  23.9 0.6 copy-start.4
  24.6 129.2 %reduce-scatter.5.cloned.1.call-start = ((), (), s32[]{:S(2)}) async-start(), calls=%async_computation.4 | async-start | bytes 81920 | tf_op jit(solution)/shard_map/reduce_scatter | solution.py:48
  97.1 130.6 %reduce-scatter.3.cloned.1.call-start = ((), (), s32[]{:S(2)}) async-start(), calls=%async_computation.3 | async-start | bytes 10485760 | tf_op jit(solution)/shard_map/reduce_scatter | solution.py:47
  111.6 150.1 %all-reduce.8.cloned.1.call-start = ((), (), s32[]{:S(2)}) async-start(), calls=%async_computation.8 | async-start | bytes 262144 | tf_op jit(solution)/shard_map/psum | solution.py:50
  117.2 201.4 %all-reduce.6.cloned.1.call-start = ((), (), s32[]{:S(2)}) async-start(), calls=%async_computation.7 | async-start | bytes 262144 | tf_op jit(solution)/shard_map/psum | solution.py:69
  155.6 236.7 %all-reduce.4.cloned.1.call-start = ((), (), s32[]{:S(2)}) async-start(), calls=%async_computation.6 | async-start | bytes 262144 | tf_op jit(solution)/shard_map/psum | solution.py:92
  244.3 6.1 %copy-start.1 = (bf16[256,2048]{1,0:T(8,128)(2,1)S(1)}, bf16[256,2048]{1,0:T(8,128)(2,1)}, u32[]{:S(2)}) copy-start(bf16[256,2048]{1,0:T(8,128)(2,1)} %param.7) | copy-start | bytes 3145732
Sparse Core Ops, SparseCore 0:
  9.6 83.4 all-gather.2
  95.8 36.3 all-gather.4
  135.2 18.5 reduce-scatter.4
  156.3 71.4 reduce-scatter.2
  229.9 31.7 all-reduce.7
  265.2 53.4 all-reduce.5
  322.6 69.7 all-reduce.3
